TPU v7x, 32 devices: a whole 2x2x4 slice. The times are simulated.
32 devices in a mesh: rows: 4 (over y, core), cols: 8 (over z, x).
Axes of the slice: x: 2, y: 2, z: 4, core: 2. Of those that a mesh axis runs over, the one named last changes fastest.
Arguments:
- tracer: float32 [384, 256, 128], P('rows', 'cols'), may hold values from 0.2 to 1.8
- crowding: float32 [384, 256, 128], P('rows', 'cols'), may hold values from 0.5 to 2
Outputs:
- potential: float32 [384, 256, 128], P('rows', 'cols')
- tracer_end: float32 [384, 256, 128], P('rows', 'cols')
All inputs are finite; a program needn't handle non-finite values.
Results may differ from a plain program's by a relative error of at most 0.00002.
Values sent between devices are 32-bit elements; how exact they have to be, the bound alone decides.
A program may use at most 64 MiB of HBM per device.

v0:
```python
import jax
import jax.numpy as jnp
from jax import lax
from jax.sharding import PartitionSpec as P

STEPS = 6


def padded_2(value, sides, width):
    for axis, dim in sides:
        size, length = (lax.axis_size(axis), value.shape[dim])
        up = [(i, (i + 1) % size) for i in range(size - 1)]
        down = [(j, i) for i, j in up]
        last = lax.slice_in_dim(value, length - width, length, axis=dim)
        leading = lax.slice_in_dim(value, 0, width, axis=dim)
        before = lax.ppermute(last, axis, up)
        after = lax.ppermute(leading, axis, down)
        value = jnp.concatenate([before, value, after], axis=dim)
    return value


def prefix(value, axis, join, neutral):
    count, mine = (lax.axis_size(axis), lax.axis_index(axis))
    pieces = lax.all_gather(value, axis)
    so_far = jnp.full_like(value, 0) + jnp.asarray(neutral, value.dtype)

    def lap(position, so_far):
        longer = join(so_far, pieces[position])
        return jnp.where(position < mine, longer, so_far)

    return lax.fori_loop(0, count - 1, lap, so_far)


def strip_edges(values, dims):
    for dim in dims:
        values = lax.slice_in_dim(values, 1, values.shape[dim] - 1, axis=dim)
    return values


def neighbour(values, dim, start, dims):
    others = [other for other in dims if other != dim]
    values = strip_edges(values, others)
    return lax.slice_in_dim(values, start, start + values.shape[dim] - 2, axis=dim)


def one_step(padded, crowding):
    middle = strip_edges(padded, (0, 1))
    lower = [neighbour(padded, dim, 0, (0, 1)) for dim in (0, 1)]
    upper = [neighbour(padded, dim, 2, (0, 1)) for dim in (0, 1)]
    spread = lower[0] + upper[0] + lower[1] + upper[1] - 4.0 * middle
    return middle + 0.1 * spread + 0.2 * middle * (1.0 - middle * crowding)


def body(tracer, crowding):
    padded = padded_2(tracer, (("rows", 0), ("cols", 1)), STEPS)
    wide_crowding = padded_2(crowding, (("rows", 0), ("cols", 1)), STEPS - 1)
    for step in range(STEPS):
        later = one_step(padded, wide_crowding)
        values = later
        margin = STEPS - 1 - step
        place = lax.axis_index("rows") * tracer.shape[0] - margin + jnp.arange(values.shape[0])
        keep_cells = (place >= 0) & (place < tracer.shape[0] * lax.axis_size("rows"))
        values = jnp.where(keep_cells.reshape((-1,) + (1,) * 2), values, 0.0)
        place = lax.axis_index("cols") * tracer.shape[1] - margin + jnp.arange(values.shape[1])
        keep_cells = (place >= 0) & (place < tracer.shape[1] * lax.axis_size("cols"))
        values = jnp.where(keep_cells.reshape((-1,) + (1,) * 1), values, 0.0)
        later = values
        if step < STEPS - 1:
            wide_crowding = strip_edges(wide_crowding, (0, 1))
        padded = later
    tracer = padded
    here = jnp.cumsum(tracer, axis=1)
    total = lax.slice_in_dim(here, here.shape[1] - 1, here.shape[1], axis=1)

    def add_pair(earlier_total, later_total):
        return earlier_total + later_total

    below = prefix(total, "cols", add_pair, jnp.zeros_like(total))
    potential = (here + below) / (tracer.shape[1] * lax.axis_size("cols"))
    return (potential, tracer)


def solution(mesh):
    return jax.shard_map(
        body,
        mesh=mesh,
        in_specs=(P("rows", "cols", None), P("rows", "cols", None)),
        out_specs=(P("rows", "cols", None), P("rows", "cols", None)),
        check_vma=False,
    )
```

profile of v0, /device:TPU:0, one launch (start us, length us, event | category | flops | bytes accessed | tf_op | source)
XLA Modules:
  0.0 116.4 jit_solution(5074464920060884348)
XLA Ops:
  0.6 1.0 fusion.48
  1.6 2.5 %collective-permute-start = (f32[6,32,128]{2,1,0:T(8,128)S(1)}, f32[6,32,128]{2,1,0:T(8,128)S(1)}, u32[]{:S(2)}, u32[]{:S(2)}) collective-permute-start(f32[6,32,128]{2,1,0:T(8,128)S(1)} %get-tuple-element.118), channel_id=1, source_target_pairs={{0,8},{8,16},{16,24},{1,9},{9,17},{17,25},{2,10},{10,18},{18,26},{... | collective-permute-start | bytes 294920 | tf_op jit(solution)/shard_map/ppermute | solution.py:16
  4.1 1.3 %collective-permute-start.1 = (f32[6,32,128]{2,1,0:T(8,128)S(1)}, f32[6,32,128]{2,1,0:T(8,128)S(1)}, u32[]{:S(2)}, u32[]{:S(2)}) collective-permute-start(f32[6,32,128]{2,1,0:T(8,128)S(1)} %get-tuple-element.117), channel_id=1, source_target_pairs={{8,0},{16,8},{24,16},{9,1},{17,9},{25,17},{10,2},{18,10},{26,18},{... | collective-permute-start | bytes 294920 | tf_op jit(solution)/shard_map/ppermute | solution.py:17
  5.4 0.9 fusion.49
  6.4 5.2 %collective-permute-start.4 = (f32[5,32,128]{2,1,0:T(8,128)S(1)}, f32[5,32,128]{2,1,0:T(8,128)S(1)}, u32[]{:S(2)}, u32[]{:S(2)}) collective-permute-start(f32[5,32,128]{2,1,0:T(8,128)S(1)} %get-tuple-element.120), channel_id=1, source_target_pairs={{0,8},{8,16},{16,24},{1,9},{9,17},{17,25},{2,10},{10,18},{18,26},{... | collective-permute-start | bytes 245768 | tf_op jit(solution)/shard_map/ppermute | solution.py:16
  11.5 1.3 %collective-permute-start.5 = (f32[5,32,128]{2,1,0:T(8,128)S(1)}, f32[5,32,128]{2,1,0:T(8,128)S(1)}, u32[]{:S(2)}, u32[]{:S(2)}) collective-permute-start(f32[5,32,128]{2,1,0:T(8,128)S(1)} %get-tuple-element.119), channel_id=1, source_target_pairs={{8,0},{16,8},{24,16},{9,1},{17,9},{25,17},{10,2},{18,10},{26,18},{... | collective-permute-start | bytes 245768 | tf_op jit(solution)/shard_map/ppermute | solution.py:17
  13.1 1.5 %constant_dynamic-update-slice_fusion.4 = f32[106,32,128]{2,1,0:T(8,128)S(1)} fusion(f32[106,32,128]{2,1,0:T(8,128)S(1)} %constant_dynamic-update-slice_fusion.5, f32[96,32,128]{2,1,0:T(8,128)} %param.5), kind=kLoop, calls=%fused_computation.78 | loop fusion | bytes 3145728
  14.6 1.4 %collective-permute-done.5 = f32[5,32,128]{2,1,0:T(8,128)S(1)} collective-permute-done((f32[5,32,128]{2,1,0:T(8,128)S(1)}, f32[5,32,128]{2,1,0:T(8,128)S(1)}, u32[]{:S(2)}, u32[]{:S(2)}) %collective-permute-start.5) | collective-permute-done | bytes 81952 | tf_op jit(solution)/shard_map/ppermute | solution.py:17
  16.2 3.4 %collective-permute-start.2 = (f32[108,6,128]{2,1,0:T(8,128)S(1)}, f32[108,6,128]{2,1,0:T(8,128)S(1)}, u32[]{:S(2)}, u32[]{:S(2)}) collective-permute-start(f32[108,6,128]{2,1,0:T(8,128)S(1)} %get-tuple-element.113), channel_id=1, source_target_pairs={{0,1},{1,2},{2,3},{3,4},{4,5},{5,6},{6,7},{8,9},{9,10},{10,11},{11... | collective-permute-start | bytes 995336 | tf_op jit(solution)/shard_map/ppermute | solution.py:16
  19.7 1.3 %collective-permute-start.3 = (f32[108,6,128]{2,1,0:T(8,128)S(1)}, f32[108,6,128]{2,1,0:T(8,128)S(1)}, u32[]{:S(2)}, u32[]{:S(2)}) collective-permute-start(f32[108,6,128]{2,1,0:T(8,128)S(1)} %get-tuple-element.114), channel_id=1, source_target_pairs={{1,0},{2,1},{3,2},{4,3},{5,4},{6,5},{7,6},{9,8},{10,9},{11,10},{12... | collective-permute-start | bytes 995336 | tf_op jit(solution)/shard_map/ppermute | solution.py:17
  21.0 4.6 %collective-permute-start.6 = (f32[106,5,128]{2,1,0:T(8,128)S(1)}, f32[106,5,128]{2,1,0:T(8,128)S(1)}, u32[]{:S(2)}, u32[]{:S(2)}) collective-permute-start(f32[106,5,128]{2,1,0:T(8,128)S(1)} %get-tuple-element.115), channel_id=1, source_target_pairs={{0,1},{1,2},{2,3},{3,4},{4,5},{5,6},{6,7},{8,9},{9,10},{10,11},{11... | collective-permute-start | bytes 814088 | tf_op jit(solution)/shard_map/ppermute | solution.py:16
  25.6 1.3 %collective-permute-start.7 = (f32[106,5,128]{2,1,0:T(8,128)S(1)}, f32[106,5,128]{2,1,0:T(8,128)S(1)}, u32[]{:S(2)}, u32[]{:S(2)}) collective-permute-start(f32[106,5,128]{2,1,0:T(8,128)S(1)} %get-tuple-element.116), channel_id=1, source_target_pairs={{1,0},{2,1},{3,2},{4,3},{5,4},{6,5},{7,6},{9,8},{10,9},{11,10},{12... | collective-permute-start | bytes 814088 | tf_op jit(solution)/shard_map/ppermute | solution.py:17
  26.9 19.9 %collective-permute-done.2 = f32[108,6,128]{2,1,0:T(8,128)S(1)} collective-permute-done((f32[108,6,128]{2,1,0:T(8,128)S(1)}, f32[108,6,128]{2,1,0:T(8,128)S(1)}, u32[]{:S(2)}, u32[]{:S(2)}) %collective-permute-start.2) | collective-permute-done | bytes 331808 | tf_op jit(solution)/shard_map/ppermute | solution.py:16
  47.3 8.9 %collective-permute-done.6 = f32[106,5,128]{2,1,0:T(8,128)S(1)} collective-permute-done((f32[106,5,128]{2,1,0:T(8,128)S(1)}, f32[106,5,128]{2,1,0:T(8,128)S(1)}, u32[]{:S(2)}, u32[]{:S(2)}) %collective-permute-start.6) | collective-permute-done | bytes 271392 | tf_op jit(solution)/shard_map/ppermute | solution.py:16
  56.1 2.8 %fusion.5 = (f32[106,42,128]{2,1,0:T(8,128)S(1)}, f32[106,42,128]{2,1,0:T(8,128)S(1)}) fusion(f32[108,44,128]{2,1,0:T(8,128)S(1)} %pad_maximum_fusion, pred[106]{0:T(512)(128)(4,1)S(1)} %compare_and_fusion, pred[42]{0:T(512)(128)(4,1)S(1)} %compare_and_fusion.1, f32[106,5,128]{2,1,0:T(8,128)S(1)} %collective-permute-done.7, ...), kind=kLoop, calls=%fused_computation.10 | loop fusion | flops 9117696 | bytes 18235540 | tf_op jit(solution)/shard_map/jit(_where)/select_n | solution.py:66
  59.0 2.2 %fusion.10 = f32[104,40,128]{2,1,0:T(8,128)S(1)} fusion(f32[106,42,128]{2,1,0:T(8,128)S(1)} %get-tuple-element.112, f32[106,42,128]{2,1,0:T(8,128)S(1)} %get-tuple-element.111, pred[104]{0:T(512)(128)(4,1)S(1)} %compare_and_fusion.2, pred[40]{0:T(512)(128)(4,1)S(1)} %compare_and_fusion.3), kind=kLoop, calls=%fused_computation.19 | loop fusion | flops 7454720 | bytes 14909584 | tf_op jit(solution)/shard_map/jit(_where)/select_n | solution.py:66
  61.1 2.2 %fusion.18 = f32[102,38,128]{2,1,0:T(8,128)S(1)} fusion(f32[106,42,128]{2,1,0:T(8,128)S(1)} %get-tuple-element.112, f32[104,40,128]{2,1,0:T(8,128)S(1)} %fusion.10, pred[102]{0:T(512)(128)(4,1)S(1)} %compare_and_fusion.4, pred[38]{0:T(512)(128)(4,1)S(1)} %compare_and_fusion.5), kind=kLoop, calls=%fused_computation.31 | loop fusion | flops 6945792 | bytes 13891724 | tf_op jit(solution)/shard_map/jit(_where)/select_n | solution.py:66
  63.4 2.2 %fusion.26 = f32[100,36,128]{2,1,0:T(8,128)S(1)} fusion(f32[106,42,128]{2,1,0:T(8,128)S(1)} %get-tuple-element.112, f32[102,38,128]{2,1,0:T(8,128)S(1)} %fusion.18, pred[100]{0:T(512)(128)(4,1)S(1)} %compare_and_fusion.6, pred[36]{0:T(512)(128)(4,1)S(1)} %compare_and_fusion.7), kind=kLoop, calls=%fused_computation.43 | loop fusion | flops 6451200 | bytes 12902536 | tf_op jit(solution)/shard_map/jit(_where)/select_n | solution.py:66
  65.6 2.1 %fusion.34 = f32[98,34,128]{2,1,0:T(8,128)S(1)} fusion(f32[106,42,128]{2,1,0:T(8,128)S(1)} %get-tuple-element.112, f32[100,36,128]{2,1,0:T(8,128)S(1)} %fusion.26, pred[98]{0:T(512)(128)(4,1)S(1)} %compare_and_fusion.8, pred[34]{0:T(512)(128)(4,1)S(1)} %compare_and_fusion.9), kind=kLoop, calls=%fused_computation.55 | loop fusion | flops 5970944 | bytes 11942020 | tf_op jit(solution)/shard_map/jit(_where)/select_n | solution.py:66
  67.7 1.6 %fusion.43 = f32[96,32,128]{2,1,0:T(8,128)S(1)} fusion(f32[98,34,128]{2,1,0:T(8,128)S(1)} %fusion.34, f32[96,32,128]{2,1,0:T(8,128)S(1)} %copy-done, pred[96]{0:T(512)(128)(4,1)S(1)} %compare_and_fusion.10, pred[32]{0:T(512)(128)(4,1)S(1)} %compare_and_fusion.11), kind=kLoop, calls=%fused_computation.68 | loop fusion | flops 5505024 | bytes 11010176 | tf_op jit(solution)/shard_map/jit(_where)/select_n | solution.py:66
  69.3 0.9 fusion.44
  70.3 37.5 %all-gather = f32[768,1,128]{2,0,1:T(8,128)} all-gather(f32[96,1,128]{2,0,1:T(8,128)S(1)} %slice.286), channel_id=2, replica_groups=mesh['rows'=4,'cols'=8] {'cols'}, dimensions={0}, use_global_device_ids=true | all-gather | bytes 442368 | tf_op jit(solution)/shard_map/all_gather | solution.py:24
  107.8 6.4 %while.14 = (s32[]{:T(128)}, f32[96,1,128]{2,1,0:T(1,128)S(1)}, s32[]{:T(128)}, f32[8,96,1,128]{3,1,2,0:T(8,128)}, s32[]{:T(128)}, /*index=5*/s32[]{:T(128)}) while((s32[]{:T(128)}, f32[96,1,128]{2,1,0:T(1,128)S(1)}, s32[]{:T(128)}, f32[8,96,1,128]{3,1,2,0:T(8,128)}, s32[]{:T(128)}, /*index=5*/s32[]{:T(128)}) %tuple.46), condition=%wide.region_2.3_spmd.clone, body=%wide.region_1.2_spmd.clone.sunk | while | flops 36868 | bytes 245853 | solution.py:31
  114.3 2.1 %copy.6 = f32[96,32,128]{2,1,0:T(8,128)} copy(f32[96,32,128]{2,0,1:T(8,128)S(1)} %add_multiply_fusion) | data formatting | bytes 3145728
  (48 shorter events, 7.3 us)
Async XLA Ops:
  1.6 14.4 %copy-start.2 = (f32[96,32,128]{2,1,0:T(8,128)S(1)}, f32[96,32,128]{2,1,0:T(8,128)}, u32[]{:S(2)}) copy-start(f32[96,32,128]{2,1,0:T(8,128)} %param.4) | copy-start | bytes 4718596
  1.6 14.4 %collective-permute-start = (f32[6,32,128]{2,1,0:T(8,128)S(1)}, f32[6,32,128]{2,1,0:T(8,128)S(1)}, u32[]{:S(2)}, u32[]{:S(2)}) collective-permute-start(f32[6,32,128]{2,1,0:T(8,128)S(1)} %get-tuple-element.118), channel_id=1, source_target_pairs={{0,8},{8,16},{16,24},{1,9},{9,17},{17,25},{2,10},{10,18},{18,26},{... | collective-permute-start | bytes 294920 | tf_op jit(solution)/shard_map/ppermute | solution.py:16
  4.1 12.0 %collective-permute-start.1 = (f32[6,32,128]{2,1,0:T(8,128)S(1)}, f32[6,32,128]{2,1,0:T(8,128)S(1)}, u32[]{:S(2)}, u32[]{:S(2)}) collective-permute-start(f32[6,32,128]{2,1,0:T(8,128)S(1)} %get-tuple-element.117), channel_id=1, source_target_pairs={{8,0},{16,8},{24,16},{9,1},{17,9},{25,17},{10,2},{18,10},{26,18},{... | collective-permute-start | bytes 294920 | tf_op jit(solution)/shard_map/ppermute | solution.py:17
  6.4 6.7 %collective-permute-start.4 = (f32[5,32,128]{2,1,0:T(8,128)S(1)}, f32[5,32,128]{2,1,0:T(8,128)S(1)}, u32[]{:S(2)}, u32[]{:S(2)}) collective-permute-start(f32[5,32,128]{2,1,0:T(8,128)S(1)} %get-tuple-element.120), channel_id=1, source_target_pairs={{0,8},{8,16},{16,24},{1,9},{9,17},{17,25},{2,10},{10,18},{18,26},{... | collective-permute-start | bytes 245768 | tf_op jit(solution)/shard_map/ppermute | solution.py:16
  11.5 4.4 %collective-permute-start.5 = (f32[5,32,128]{2,1,0:T(8,128)S(1)}, f32[5,32,128]{2,1,0:T(8,128)S(1)}, u32[]{:S(2)}, u32[]{:S(2)}) collective-permute-start(f32[5,32,128]{2,1,0:T(8,128)S(1)} %get-tuple-element.119), channel_id=1, source_target_pairs={{8,0},{16,8},{24,16},{9,1},{17,9},{25,17},{10,2},{18,10},{26,18},{... | collective-permute-start | bytes 245768 | tf_op jit(solution)/shard_map/ppermute | solution.py:17
  16.2 30.6 %collective-permute-start.2 = (f32[108,6,128]{2,1,0:T(8,128)S(1)}, f32[108,6,128]{2,1,0:T(8,128)S(1)}, u32[]{:S(2)}, u32[]{:S(2)}) collective-permute-start(f32[108,6,128]{2,1,0:T(8,128)S(1)} %get-tuple-element.113), channel_id=1, source_target_pairs={{0,1},{1,2},{2,3},{3,4},{4,5},{5,6},{6,7},{8,9},{9,10},{10,11},{11... | collective-permute-start | bytes 995336 | tf_op jit(solution)/shard_map/ppermute | solution.py:16
  19.7 27.2 %collective-permute-start.3 = (f32[108,6,128]{2,1,0:T(8,128)S(1)}, f32[108,6,128]{2,1,0:T(8,128)S(1)}, u32[]{:S(2)}, u32[]{:S(2)}) collective-permute-start(f32[108,6,128]{2,1,0:T(8,128)S(1)} %get-tuple-element.114), channel_id=1, source_target_pairs={{1,0},{2,1},{3,2},{4,3},{5,4},{6,5},{7,6},{9,8},{10,9},{11,10},{12... | collective-permute-start | bytes 995336 | tf_op jit(solution)/shard_map/ppermute | solution.py:17
  21.0 35.1 %collective-permute-start.6 = (f32[106,5,128]{2,1,0:T(8,128)S(1)}, f32[106,5,128]{2,1,0:T(8,128)S(1)}, u32[]{:S(2)}, u32[]{:S(2)}) collective-permute-start(f32[106,5,128]{2,1,0:T(8,128)S(1)} %get-tuple-element.115), channel_id=1, source_target_pairs={{0,1},{1,2},{2,3},{3,4},{4,5},{5,6},{6,7},{8,9},{9,10},{10,11},{11... | collective-permute-start | bytes 814088 | tf_op jit(solution)/shard_map/ppermute | solution.py:16
  25.6 30.5 %collective-permute-start.7 = (f32[106,5,128]{2,1,0:T(8,128)S(1)}, f32[106,5,128]{2,1,0:T(8,128)S(1)}, u32[]{:S(2)}, u32[]{:S(2)}) collective-permute-start(f32[106,5,128]{2,1,0:T(8,128)S(1)} %get-tuple-element.116), channel_id=1, source_target_pairs={{1,0},{2,1},{3,2},{4,3},{5,4},{6,5},{7,6},{9,8},{10,9},{11,10},{12... | collective-permute-start | bytes 814088 | tf_op jit(solution)/shard_map/ppermute | solution.py:17
  65.5 2.2 %copy-start = (f32[96,32,128]{2,1,0:T(8,128)S(1)}, f32[96,32,128]{2,1,0:T(8,128)}, u32[]{:S(2)}) copy-start(f32[96,32,128]{2,1,0:T(8,128)} %param.5) | copy-start | bytes 4718596
  69.3 38.5 %copy-start.1 = (f32[96,32,128]{2,1,0:T(8,128)}, f32[96,32,128]{2,1,0:T(8,128)S(1)}, u32[]{:S(2)}) copy-start(f32[96,32,128]{2,1,0:T(8,128)S(1)} %fusion.43) | copy-start | bytes 4718596
where the time goes:
time: 117 us; the launch traced here: 116 us
  blocking collectives  37.5 us (32%)
  waiting for transfers between devices  30.2 us (26%)
  starting transfers between devices  20.9 us (18%)
  other arithmetic  15.4 us (13%)
  local copies, waits for them, and re-layouts  11.4 us (10%)
    all_gather x1, blocking collectives, prefix(): pieces = lax.all_gather(value, axis)  37.5 us
    ppermute x4, waiting for transfers between devices, padded_2(): before = lax.ppermute(last, axis, up)  28.8 us
    ppermute x4, starting transfers between devices, padded_2(): before = lax.ppermute(last, axis, up)  15.7 us
    select_n x6, other arithmetic, body(): values = jnp.where(keep_cells.reshape((-1,) + (1,) * 1), values, 0.0)  13.1 us
    dynamic_slice x7, local copies, waits for them, and re-layouts, lap(): longer = join(so_far, pieces[position])  5.64 us
    ppermute x4, starting transfers between devices, padded_2(): after = lax.ppermute(leading, axis, down)  5.17 us
    unnamed x11, local copies, waits for them, and re-layouts  3.74 us
  transfers between devices with their start and end apart: 8, of which 3 were waited for; matrix products, arithmetic and copies ran while one was open for 3% of the time, Pallas kernels for 0%

commit v1 on v0

v1 whole, which is shorter than its diff:
```python
import functools

import jax
import jax.numpy as jnp
from jax import lax
from jax.experimental import pallas as pl
from jax.experimental.pallas import tpu as pltpu
from jax.sharding import PartitionSpec as P

STEPS = 6
MESH = pl.DeviceIdType.MESH
LANES = 8


def chunk_rows(height):
    for rows in (16, 24, 32, 8):
        if height % rows == 0:
            return rows
    return height


def kernel(
    sizes, t_hbm, c_hbm, pot_hbm, end_hbm,
    buf, crowd, pot, col_send, col_recv, row_send, row_recv,
    total, pair_recv, pair_sum, group_recv,
    load_t, load_c, store_pot, store_end,
    col_ssem, col_rsem, row_ssem, row_rsem,
    pair_ssem, pair_rsem, group_ssem, group_rsem,
):
    height, width, n_rows, n_cols = sizes
    rc = chunk_rows(height)
    chunks = height // rc
    inner = 2 if n_cols % 2 == 0 else 1
    groups = n_cols // inner
    unroll = 8
    row, col = lax.axis_index("rows"), lax.axis_index("cols")
    member, group = lax.rem(col, inner), lax.div(col, inner)
    zero8 = jnp.zeros((LANES, buf.shape[-1]), jnp.float32)

    def at_col(c):
        return {"rows": row, "cols": c}

    def at_row(r):
        return {"rows": r, "cols": col}

    loads = []
    for r in range(chunks):
        part = pl.ds(r * rc * width, rc * width)
        loads.append(pltpu.make_async_copy(
            t_hbm.at[part], buf.at[0, pl.ds((1 + r * rc) * width, rc * width)], load_t.at[r]))
    for load in loads:
        load.start()
    crowd_loads = []
    for r in range(chunks):
        part = pl.ds(r * rc * width, rc * width)
        crowd_loads.append(pltpu.make_async_copy(c_hbm.at[part], crowd.at[part], load_c.at[r]))
    for load in crowd_loads:
        load.start()

    barrier = pltpu.get_barrier_semaphore()

    def greet(there, device):
        @pl.when(there)
        def _():
            pl.semaphore_signal(barrier, inc=1, device_id=device, device_id_type=MESH)
        return there.astype(jnp.int32)

    has_left, has_right = col > 0, col < n_cols - 1
    has_up, has_down = row > 0, row < n_rows - 1
    met = greet(has_left, at_col(col - 1)) + greet(has_right, at_col(col + 1))
    met += greet(has_up, at_row(row - 1)) + greet(has_down, at_row(row + 1))
    for gap in range(1, groups):
        if gap * inner == 1:
            continue
        met += greet(group >= gap, at_col(col - gap * inner))
        met += greet(group + gap < groups, at_col(col + gap * inner))

    for side, there in ((0, has_left), (1, has_right)):
        @pl.when(jnp.logical_not(there))
        def _():
            @pl.loop(0, STEPS * height // LANES)
            def _(i):
                s, y = lax.div(i, height // LANES), lax.rem(i, height // LANES)
                col_recv[s, side, pl.ds(pl.multiple_of(y * LANES, LANES), LANES)] = zero8
    for side, there in ((0, has_up), (1, has_down)):
        @pl.when(jnp.logical_not(there))
        def _():
            @pl.loop(0, STEPS * width // LANES)
            def _(i):
                s, x = lax.div(i, width // LANES), lax.rem(i, width // LANES)
                row_recv[s, side, pl.ds(pl.multiple_of(x * LANES, LANES), LANES)] = zero8

    pl.semaphore_wait(barrier, met)

    def col_copy(s, side, r):
        rows = pl.ds(r * rc, rc)
        return pltpu.make_async_remote_copy(
            src_ref=col_send.at[s, side, rows], dst_ref=col_recv.at[s, 1 - side, rows],
            send_sem=col_ssem.at[s, side, r], recv_sem=col_rsem.at[s, 1 - side, r],
            device_id=at_col(col - 1 if side == 0 else col + 1), device_id_type=MESH)

    def col_arrival(s, side, r):
        rows = pl.ds(r * rc, rc)
        return pltpu.make_async_remote_copy(
            src_ref=col_send.at[s, side, rows], dst_ref=col_recv.at[s, side, rows],
            send_sem=col_ssem.at[s, side, r], recv_sem=col_rsem.at[s, side, r],
            device_id=at_col(col - 1 if side == 0 else col + 1), device_id_type=MESH)

    def row_copy(s, side):
        return pltpu.make_async_remote_copy(
            src_ref=row_send.at[s, side], dst_ref=row_recv.at[s, 1 - side],
            send_sem=row_ssem.at[s, side], recv_sem=row_rsem.at[s, 1 - side],
            device_id=at_row(row - 1 if side == 0 else row + 1), device_id_type=MESH)

    def row_arrival(s, side):
        return pltpu.make_async_remote_copy(
            src_ref=row_send.at[s, side], dst_ref=row_recv.at[s, side],
            send_sem=row_ssem.at[s, side], recv_sem=row_rsem.at[s, side],
            device_id=at_row(row - 1 if side == 0 else row + 1), device_id_type=MESH)

    def send_edges(p, s, r):
        for side, x in ((0, 0), (1, width - 1)):
            for y in range(r * rc, r * rc + rc, LANES):
                col_send[s, side, pl.ds(y, LANES)] = buf[p, pl.ds((1 + y) * width + x, LANES, stride=width)]
        for side, y, there in ((0, 0, has_up), (1, height - 1, has_down)):
            if r == y // rc:
                @pl.when(there)
                def _():
                    row_send[s, side] = buf[p, pl.ds((1 + y) * width, width)]
                    row_copy(s, side).start()
        for side, there in ((0, has_left), (1, has_right)):
            @pl.when(there)
            def _():
                col_copy(s, side, r).start()

    for r in range(chunks):
        loads[r].wait()
        send_edges(0, 0, r)
    for r in range(chunks):
        crowd_loads[r].wait()

        @pl.loop(0, rc * width // (LANES * 8))
        def _(i):
            at = pl.ds(pl.multiple_of(r * rc * width + i * LANES * 8, LANES * 8), LANES * 8)
            crowd[at] = crowd[at] * 0.2

    place = lax.broadcasted_iota(jnp.int32, (LANES, buf.shape[-1]), 0)
    tiles = width // LANES

    def compute(p, q, s, r):
        for side, y, at in ((0, 0, 0), (1, height - 1, height + 1)):
            if r == y // rc:
                @pl.when((has_up, has_down)[side])
                def _():
                    row_arrival(s, side).wait_recv()
                buf[p, pl.ds(at * width, width)] = row_recv[s, side]
        for side, there in ((0, has_left), (1, has_right)):
            @pl.when(there)
            def _():
                col_arrival(s, side, r).wait_recv()

        @pl.loop(0, rc // unroll)
        def _(i):
            y0 = r * rc + i * unroll
            for j in range(tiles):
                o = pl.multiple_of((1 + y0) * width + j * LANES, LANES)
                rows = [buf[p, pl.ds(o + (u - 1) * width, LANES)] for u in range(unroll + 2)]
                for u in range(unroll):
                    middle = rows[u + 1]
                    before = buf[p, pl.ds(o + u * width - 1, LANES)]
                    after = buf[p, pl.ds(o + u * width + 1, LANES)]
                    if j == 0:
                        edge = jnp.broadcast_to(col_recv[s, 0, pl.ds(y0 + u, 1)], before.shape)
                        before = jnp.where(place == 0, edge, before)
                    if j == tiles - 1:
                        edge = jnp.broadcast_to(col_recv[s, 1, pl.ds(y0 + u, 1)], before.shape)
                        after = jnp.where(place == LANES - 1, edge, after)
                    c = crowd[pl.ds(o + (u - 1) * width, LANES)]
                    around = (rows[u] + rows[u + 2]) + (before + after)
                    buf[q, pl.ds(o + u * width, LANES)] = 0.1 * around + middle * (0.8 - middle * c)

    @pl.loop(0, STEPS - 1)
    def _(s):
        p = lax.rem(s, 2)
        for r in range(chunks):
            compute(p, 1 - p, s, r)
            send_edges(1 - p, s + 1, r)

    p, q = (STEPS - 1) % 2, STEPS % 2
    pair_to = col + 1 - 2 * member

    def pair_copy(r):
        rows = pl.ds(r * rc, rc)
        return pltpu.make_async_remote_copy(
            src_ref=total.at[rows], dst_ref=pair_recv.at[rows],
            send_sem=pair_ssem.at[r], recv_sem=pair_rsem.at[r],
            device_id=at_col(pair_to), device_id_type=MESH)

    def group_copy(gap, r):
        rows = pl.ds(r * rc, rc)
        return pltpu.make_async_remote_copy(
            src_ref=pair_sum.at[rows], dst_ref=group_recv.at[gap, rows],
            send_sem=group_ssem.at[gap, r], recv_sem=group_rsem.at[gap, r],
            device_id=at_col(col + gap * inner), device_id_type=MESH)

    def end_copy(r):
        return pltpu.make_async_copy(
            buf.at[q, pl.ds((1 + r * rc) * width, rc * width)],
            end_hbm.at[pl.ds(r * rc * width, rc * width)], store_end.at[r])

    def pot_copy(r):
        part = pl.ds(r * rc * width, rc * width)
        return pltpu.make_async_copy(pot.at[part], pot_hbm.at[part], store_pot.at[r])

    for r in range(chunks):
        compute(p, q, STEPS - 1, r)
        end_copy(r).start()

        @pl.loop(0, rc // LANES)
        def _(i):
            y = pl.multiple_of(r * rc + i * LANES, LANES)
            so_far = zero8
            for x in range(width):
                so_far = so_far + buf[q, pl.ds((1 + y) * width + x, LANES, stride=width)]
                pot[pl.ds(y * width + x, LANES, stride=width)] = so_far
            total[pl.ds(y, LANES)] = so_far
        if inner == 2:
            pair_copy(r).start()

    for r in range(chunks):
        rows = pl.ds(r * rc, rc)
        if inner == 2:
            pair_copy(r).wait_recv()
            pair_sum[rows] = total[rows] + pair_recv[rows]
        else:
            pair_sum[rows] = total[rows]
        for gap in range(1, groups):
            @pl.when(group + gap < groups)
            def _():
                group_copy(gap, r).start()

    scale = 1.0 / (width * n_cols)
    for r in range(chunks):
        rows = pl.ds(r * rc, rc)
        if inner == 2:
            pair_copy(r).wait_send()
            total[rows] = pair_recv[rows] * member.astype(jnp.float32)
        else:
            total[rows] = jnp.zeros((rc, buf.shape[-1]), jnp.float32)
        for gap in range(1, groups):
            @pl.when(group >= gap)
            def _():
                group_copy(gap, r).wait_recv()
                total[rows] += group_recv[gap, rows]

        @pl.loop(0, rc // LANES)
        def _(i):
            y = pl.multiple_of(r * rc + i * LANES, LANES)
            below = total[pl.ds(y, LANES)]
            for x in range(width):
                at = pl.ds(y * width + x, LANES, stride=width)
                pot[at] = (pot[at] + below) * scale
        pot_copy(r).start()

    for r in range(chunks):
        end_copy(r).wait()
        pot_copy(r).wait()

    @pl.loop(0, STEPS)
    def _(s):
        for side, there in ((0, has_left), (1, has_right)):
            @pl.when(there)
            def _():
                for r in range(chunks):
                    col_copy(s, side, r).wait_send()
        for side, there in ((0, has_up), (1, has_down)):
            @pl.when(there)
            def _():
                row_copy(s, side).wait_send()
    for gap in range(1, groups):
        @pl.when(group + gap < groups)
        def _():
            for r in range(chunks):
                group_copy(gap, r).wait_send()


def body(tracer, crowding):
    height, width, members = tracer.shape
    n_rows, n_cols = lax.axis_size("rows"), lax.axis_size("cols")
    chunks = height // chunk_rows(height)
    groups = n_cols // 2 if n_cols % 2 == 0 else n_cols
    cells = height * width
    f32 = jnp.float32
    dma = pltpu.SemaphoreType.DMA
    out = jax.ShapeDtypeStruct((cells, members), f32)
    potential, end = pl.pallas_call(
        functools.partial(kernel, (height, width, n_rows, n_cols)),
        out_shape=(out, out),
        in_specs=[pl.BlockSpec(memory_space=pl.ANY)] * 2,
        out_specs=[pl.BlockSpec(memory_space=pl.ANY)] * 2,
        scratch_shapes=[
            pltpu.VMEM((2, (height + 2) * width, members), f32),
            pltpu.VMEM((cells, members), f32),
            pltpu.VMEM((cells, members), f32),
            pltpu.VMEM((STEPS, 2, height, members), f32),
            pltpu.VMEM((STEPS, 2, height, members), f32),
            pltpu.VMEM((STEPS, 2, width, members), f32),
            pltpu.VMEM((STEPS, 2, width, members), f32),
            pltpu.VMEM((height, members), f32),
            pltpu.VMEM((height, members), f32),
            pltpu.VMEM((height, members), f32),
            pltpu.VMEM((groups, height, members), f32),
            dma((chunks,)), dma((chunks,)), dma((chunks,)), dma((chunks,)),
            dma((STEPS, 2, chunks)), dma((STEPS, 2, chunks)),
            dma((STEPS, 2)), dma((STEPS, 2)),
            dma((chunks,)), dma((chunks,)),
            dma((groups, chunks)), dma((groups, chunks)),
        ],
        compiler_params=pltpu.CompilerParams(collective_id=0, has_side_effects=True),
    )(tracer.reshape(cells, members), crowding.reshape(cells, members))
    return potential.reshape(tracer.shape), end.reshape(tracer.shape)


def solution(mesh):
    return jax.shard_map(
        body,
        mesh=mesh,
        in_specs=(P("rows", "cols", None), P("rows", "cols", None)),
        out_specs=(P("rows", "cols", None), P("rows", "cols", None)),
        check_vma=False,
    )
```

time: 117 us -> 41.7 us (0.36)
  blocking collectives: 37.5 us -> 0 us
  Pallas kernels: 0 us -> 36.7 us
  waiting for transfers between devices: 30.2 us -> 0 us
  starting transfers between devices: 20.9 us -> 0 us
  other arithmetic: 15.4 us -> 0 us
  local copies, waits for them, and re-layouts: 11.4 us -> 3.93 us
    all_gather x1 -> x0, blocking collectives: 37.5 us -> none  [prefix(): pieces = lax.all_gather(value, axis)]
    pallas_call x0 -> x1, Pallas kernels: none -> 36.7 us  [body(): pl.pallas_call(functools.partial(kernel, (height, width, n_rows, n_cols))...]
    ppermute x8 -> x0, waiting for transfers between devices: 30.2 us -> none  [the longest x4 28.8 us: padded_2(): before = lax.ppermute(last, axis, up)]
    ppermute x8 -> x0, starting transfers between devices: 20.9 us -> none  [the longest x4 15.7 us: padded_2(): before = lax.ppermute(last, axis, up)]
    select_n x13 -> x0, other arithmetic: 13.8 us -> none  [the longest x6 13.1 us: body(): values = jnp.where(keep_cells.reshape((-1,) + (1,) * 1), values, 0.0)]
    dynamic_slice x7 -> x0, local copies, waits for them, and re-layouts: 5.64 us -> none  [lap(): longer = join(so_far, pieces[position])]
    slice x5 -> x0, local copies, waits for them, and re-layouts: 2.02 us -> none  [the longest x2 1.9 us: padded_2(): leading = lax.slice_in_dim(value, 0, width, axis=dim)]
    unnamed x11 -> x4, local copies, waits for them, and re-layouts: 3.74 us -> 3.93 us
  transfers between devices with their start and end apart: 8 -> 0, of which waited for: 3 -> 0; matrix products, arithmetic and copies ran while one was open for 3% -> 0% of each run, Pallas kernels for 0% -> 0%
where the time goes in v1:
time: 41.7 us; the launch traced here: 41.3 us
  Pallas kernels  36.7 us (88%)
  local copies, waits for them, and re-layouts  3.93 us (9%)
  between operations  0.65 us (2%)
    pallas_call x1, Pallas kernels, body(): pl.pallas_call(functools.partial(kernel, (height, width, n_rows, n_cols))...  36.7 us
    unnamed x4, local copies, waits for them, and re-layouts  3.93 us

profile of v1, /device:TPU:0, one launch (start us, length us, event | category | flops | bytes accessed | tf_op | source)
XLA Modules:
  0.0 41.3 jit_solution(7974102301084649770)
XLA Ops:
  0.6 36.7 %shard_map.41 = (f32[3072,128]{1,0:T(8,128)}, f32[3072,128]{1,0:T(8,128)}) custom-call(f32[3072,128]{1,0:T(8,128)} %bitcast.4, f32[3072,128]{1,0:T(8,128)} %bitcast.5), custom_call_target="tpu_custom_call" | custom-call | tf_op jit(solution)/shard_map/pallas_call | solution.py:296
  37.4 0.0 copy-start
  37.4 2.8 %copy.6 = f32[96,32,128]{2,1,0:T(8,128)} copy(f32[96,32,128]{2,1,0:T(8,128)} %bitcast.7) | data formatting | bytes 3145728
  40.2 0.0 copy-done
  40.2 1.1 %copy.7 = f32[96,32,128]{2,1,0:T(8,128)} copy(f32[96,32,128]{2,1,0:T(8,128)S(1)} %bitcast.6) | data formatting | bytes 3145728
Async XLA Ops:
  37.4 2.8 %copy-start = (f32[3072,128]{1,0:T(8,128)S(1)}, f32[3072,128]{1,0:T(8,128)}, u32[]{:S(2)}) copy-start(f32[3072,128]{1,0:T(8,128)} %get-tuple-element.5) | copy-start | bytes 4718596

commit v2 on v1

--- a/solution.py
+++ b/solution.py
@@ -10,6 +10,7 @@
 STEPS = 6
 MESH = pl.DeviceIdType.MESH
 LANES = 8
+GRANT = 24 * 2**20
 
 
 def chunk_rows(height):
@@ -20,10 +21,10 @@
 
 
 def kernel(
-    sizes, t_hbm, c_hbm, pot_hbm, end_hbm,
-    buf, crowd, pot, col_send, col_recv, row_send, row_recv,
+    sizes, t_hbm, c_hbm, end, here, below,
+    buf, crowd, col_send, col_recv, row_send, row_recv,
     total, pair_recv, pair_sum, group_recv,
-    load_t, load_c, store_pot, store_end,
+    load_t, load_c,
     col_ssem, col_rsem, row_ssem, row_rsem,
     pair_ssem, pair_rsem, group_ssem, group_rsem,
 ):
@@ -147,7 +148,7 @@
     place = lax.broadcasted_iota(jnp.int32, (LANES, buf.shape[-1]), 0)
     tiles = width // LANES
 
-    def compute(p, q, s, r):
+    def compute(p, q, s, r, last=False):
         for side, y, at in ((0, 0, 0), (1, height - 1, height + 1)):
             if r == y // rc:
                 @pl.when((has_up, has_down)[side])
@@ -162,22 +163,34 @@
         @pl.loop(0, rc // unroll)
         def _(i):
             y0 = r * rc + i * unroll
-            for j in range(tiles):
-                o = pl.multiple_of((1 + y0) * width + j * LANES, LANES)
-                rows = [buf[p, pl.ds(o + (u - 1) * width, LANES)] for u in range(unroll + 2)]
-                for u in range(unroll):
-                    middle = rows[u + 1]
-                    before = buf[p, pl.ds(o + u * width - 1, LANES)]
-                    after = buf[p, pl.ds(o + u * width + 1, LANES)]
-                    if j == 0:
-                        edge = jnp.broadcast_to(col_recv[s, 0, pl.ds(y0 + u, 1)], before.shape)
-                        before = jnp.where(place == 0, edge, before)
-                    if j == tiles - 1:
-                        edge = jnp.broadcast_to(col_recv[s, 1, pl.ds(y0 + u, 1)], before.shape)
-                        after = jnp.where(place == LANES - 1, edge, after)
-                    c = crowd[pl.ds(o + (u - 1) * width, LANES)]
-                    around = (rows[u] + rows[u + 2]) + (before + after)
-                    buf[q, pl.ds(o + u * width, LANES)] = 0.1 * around + middle * (0.8 - middle * c)
+            base = pl.multiple_of((1 + y0) * width, LANES)
+
+            def line(u):
+                return [buf[p, pl.ds(base + u * width + j * LANES, LANES)] for j in range(tiles)]
+
+            above, middle = line(-1), line(0)
+            for u in range(unroll):
+                under = line(u + 1)
+                forth = [pltpu.roll(m, 1, 0) for m in middle]
+                back = [pltpu.roll(m, LANES - 1, 0) for m in middle]
+                first = jnp.broadcast_to(col_recv[s, 0, pl.ds(y0 + u, 1)], zero8.shape)
+                final = jnp.broadcast_to(col_recv[s, 1, pl.ds(y0 + u, 1)], zero8.shape)
+                news = []
+                for j in range(tiles):
+                    before = jnp.where(place == 0, forth[j - 1] if j else first, forth[j])
+                    after = jnp.where(place == LANES - 1, back[j + 1] if j + 1 < tiles else final, back[j])
+                    c = crowd[pl.ds(base + (u - 1) * width + j * LANES, LANES)]
+                    around = (above[j] + under[j]) + (before + after)
+                    new = 0.1 * around + middle[j] * (0.8 - middle[j] * c)
+                    news.append(new)
+                    if last:
+                        end[pl.ds(base + (u - 1) * width + j * LANES, LANES)] = new
+                    else:
+                        buf[q, pl.ds(base + u * width + j * LANES, LANES)] = new
+                if last:
+                    whole = functools.reduce(jnp.add, news)
+                    total[pl.ds(y0 + u, 1)] = jnp.sum(whole, axis=0, keepdims=True)
+                above, middle = middle, under
 
     @pl.loop(0, STEPS - 1)
     def _(s):
@@ -203,29 +216,24 @@
             send_sem=group_ssem.at[gap, r], recv_sem=group_rsem.at[gap, r],
             device_id=at_col(col + gap * inner), device_id_type=MESH)
 
-    def end_copy(r):
-        return pltpu.make_async_copy(
-            buf.at[q, pl.ds((1 + r * rc) * width, rc * width)],
-            end_hbm.at[pl.ds(r * rc * width, rc * width)], store_end.at[r])
-
-    def pot_copy(r):
-        part = pl.ds(r * rc * width, rc * width)
-        return pltpu.make_async_copy(pot.at[part], pot_hbm.at[part], store_pot.at[r])
-
-    for r in range(chunks):
-        compute(p, q, STEPS - 1, r)
-        end_copy(r).start()
-
+    def sum_along(r):
         @pl.loop(0, rc // LANES)
         def _(i):
             y = pl.multiple_of(r * rc + i * LANES, LANES)
             so_far = zero8
             for x in range(width):
-                so_far = so_far + buf[q, pl.ds((1 + y) * width + x, LANES, stride=width)]
-                pot[pl.ds(y * width + x, LANES, stride=width)] = so_far
-            total[pl.ds(y, LANES)] = so_far
+                at = pl.ds(y * width + x, LANES, stride=width)
+                so_far = so_far + end[at]
+                here[at] = so_far
+
+    for r in range(chunks):
+        compute(p, q, STEPS - 1, r, last=True)
         if inner == 2:
             pair_copy(r).start()
+
+    early = chunks // 2
+    for r in range(early):
+        sum_along(r)
 
     for r in range(chunks):
         rows = pl.ds(r * rc, rc)
@@ -239,32 +247,21 @@
             def _():
                 group_copy(gap, r).start()
 
-    scale = 1.0 / (width * n_cols)
+    for r in range(early, chunks):
+        sum_along(r)
+
     for r in range(chunks):
         rows = pl.ds(r * rc, rc)
         if inner == 2:
             pair_copy(r).wait_send()
-            total[rows] = pair_recv[rows] * member.astype(jnp.float32)
+            below[rows] = pair_recv[rows] * member.astype(jnp.float32)
         else:
-            total[rows] = jnp.zeros((rc, buf.shape[-1]), jnp.float32)
+            below[rows] = jnp.zeros((rc, buf.shape[-1]), jnp.float32)
         for gap in range(1, groups):
             @pl.when(group >= gap)
             def _():
                 group_copy(gap, r).wait_recv()
-                total[rows] += group_recv[gap, rows]
-
-        @pl.loop(0, rc // LANES)
-        def _(i):
-            y = pl.multiple_of(r * rc + i * LANES, LANES)
-            below = total[pl.ds(y, LANES)]
-            for x in range(width):
-                at = pl.ds(y * width + x, LANES, stride=width)
-                pot[at] = (pot[at] + below) * scale
-        pot_copy(r).start()
-
-    for r in range(chunks):
-        end_copy(r).wait()
-        pot_copy(r).wait()
+                below[rows] += group_recv[gap, rows]
 
     @pl.loop(0, STEPS)
     def _(s):
@@ -282,6 +279,32 @@
         def _():
             for r in range(chunks):
                 group_copy(gap, r).wait_send()
+
+
+def finish(sizes, end, here, below, pot_hbm, end_hbm, pot, pot_sem, end_sem):
+    height, width, n_cols = sizes
+    rc = chunk_rows(height)
+    end_copy = pltpu.make_async_copy(end, end_hbm, end_sem)
+    end_copy.start()
+    scale = 1.0 / (width * n_cols)
+
+    def pot_copy(r):
+        part = pl.ds(r * rc * width, rc * width)
+        return pltpu.make_async_copy(pot.at[part], pot_hbm.at[part], pot_sem.at[r])
+
+    for r in range(height // rc):
+        @pl.loop(0, rc // LANES)
+        def _(i):
+            for u in range(LANES):
+                y = r * rc + i * LANES + u
+                earlier = jnp.broadcast_to(below[pl.ds(y, 1)], (LANES, pot.shape[-1]))
+                for x in range(0, width, LANES):
+                    at = pl.ds(pl.multiple_of(y * width + x, LANES), LANES)
+                    pot[at] = (here[at] + earlier) * scale
+        pot_copy(r).start()
+    end_copy.wait()
+    for r in range(height // rc):
+        pot_copy(r).wait()
 
 
 def body(tracer, crowding):
@@ -293,14 +316,17 @@
     f32 = jnp.float32
     dma = pltpu.SemaphoreType.DMA
     out = jax.ShapeDtypeStruct((cells, members), f32)
-    potential, end = pl.pallas_call(
+    end, here, below = pl.pallas_call(
         functools.partial(kernel, (height, width, n_rows, n_cols)),
-        out_shape=(out, out),
-        in_specs=[pl.BlockSpec(memory_space=pl.ANY)] * 2,
-        out_specs=[pl.BlockSpec(memory_space=pl.ANY)] * 2,
+        out_shape=(
+            pltpu.VMEM((cells, members), f32),
+            pltpu.VMEM((cells, members), f32),
+            pltpu.VMEM((height, members), f32),
+        ),
+        in_specs=[pl.BlockSpec(memory_space=pltpu.HBM)] * 2,
+        out_specs=[pl.BlockSpec(memory_space=pltpu.VMEM)] * 3,
         scratch_shapes=[
             pltpu.VMEM((2, (height + 2) * width, members), f32),
-            pltpu.VMEM((cells, members), f32),
             pltpu.VMEM((cells, members), f32),
             pltpu.VMEM((STEPS, 2, height, members), f32),
             pltpu.VMEM((STEPS, 2, height, members), f32),
@@ -310,14 +336,23 @@
             pltpu.VMEM((height, members), f32),
             pltpu.VMEM((height, members), f32),
             pltpu.VMEM((groups, height, members), f32),
-            dma((chunks,)), dma((chunks,)), dma((chunks,)), dma((chunks,)),
+            dma((chunks,)), dma((chunks,)),
             dma((STEPS, 2, chunks)), dma((STEPS, 2, chunks)),
             dma((STEPS, 2)), dma((STEPS, 2)),
             dma((chunks,)), dma((chunks,)),
             dma((groups, chunks)), dma((groups, chunks)),
         ],
-        compiler_params=pltpu.CompilerParams(collective_id=0, has_side_effects=True),
+        compiler_params=pltpu.CompilerParams(
+            collective_id=0, has_side_effects=True, vmem_limit_bytes=GRANT),
     )(tracer.reshape(cells, members), crowding.reshape(cells, members))
+    potential, end = pl.pallas_call(
+        functools.partial(finish, (height, width, n_cols)),
+        out_shape=(out, out),
+        in_specs=[pl.BlockSpec(memory_space=pltpu.VMEM)] * 3,
+        out_specs=[pl.BlockSpec(memory_space=pl.ANY)] * 2,
+        scratch_shapes=[pltpu.VMEM((cells, members), f32), dma((chunks,)), dma],
+        compiler_params=pltpu.CompilerParams(vmem_limit_bytes=GRANT),
+    )(end, here, below)
     return potential.reshape(tracer.shape), end.reshape(tracer.shape)
 
 

time: 41.7 us -> 38.2 us (0.916)
  Pallas kernels: 36.7 us -> 34.6 us
  local copies, waits for them, and re-layouts: 3.93 us -> 2.81 us
    pallas_call x1, Pallas kernels: 36.7 us -> 32.8 us  [body(): pl.pallas_call(functools.partial(kernel, (height, width, n_rows, n_cols))...]
    pallas_call x0 -> x1, Pallas kernels: none -> 1.71 us  [body(): pl.pallas_call(functools.partial(finish, (height, width, n_cols)), out_sh...]
    unnamed x4, local copies, waits for them, and re-layouts: 3.93 us -> 2.81 us
where the time goes in v2:
time: 38.2 us; the launch traced here: 38 us
  Pallas kernels  34.6 us (91%)
  local copies, waits for them, and re-layouts  2.81 us (7%)
  between operations  0.65 us (2%)
    pallas_call x1, Pallas kernels, body(): pl.pallas_call(functools.partial(kernel, (height, width, n_rows, n_cols))...  32.8 us
    unnamed x4, local copies, waits for them, and re-layouts  2.81 us
    pallas_call x1, Pallas kernels, body(): pl.pallas_call(functools.partial(finish, (height, width, n_cols)), out_sh...  1.71 us

profile of v2, /device:TPU:0, one launch (start us, length us, event | category | flops | bytes accessed | tf_op | source)
XLA Modules:
  0.0 38.0 jit_solution(12918198464597703430)
XLA Ops:
  0.6 0.0 copy-start
  0.6 1.4 %copy-done = f32[96,32,128]{2,1,0:T(8,128)S(1)} copy-done((f32[96,32,128]{2,1,0:T(8,128)S(1)}, f32[96,32,128]{2,1,0:T(8,128)}, u32[]{:S(2)}) %copy-start) | copy-done | bytes 1572888
  2.0 0.0 copy-start.1
  2.0 1.4 %copy-done.1 = f32[96,32,128]{2,1,0:T(8,128)S(1)} copy-done((f32[96,32,128]{2,1,0:T(8,128)S(1)}, f32[96,32,128]{2,1,0:T(8,128)}, u32[]{:S(2)}) %copy-start.1) | copy-done | bytes 1572888
  3.4 32.8 %shard_map.41 = (f32[3072,128]{1,0:T(8,128)S(1)}, f32[3072,128]{1,0:T(8,128)S(1)}, f32[96,128]{1,0:T(8,128)S(1)}) custom-call(f32[3072,128]{1,0:T(8,128)S(1)} %bitcast.4, f32[3072,128]{1,0:T(8,128)S(1)} %bitcast.5), custom_call_target="tpu_custom_call" | custom-call | tf_op jit(solution)/shard_map/pallas_call | solution.py:319
  36.3 1.7 %shard_map.42 = (f32[3072,128]{1,0:T(8,128)}, f32[3072,128]{1,0:T(8,128)}) custom-call(f32[3072,128]{1,0:T(8,128)S(1)} %get-tuple-element.7.end, f32[3072,128]{1,0:T(8,128)S(1)} %get-tuple-element.8.here, f32[96,128]{1,0:T(8,128)S(1)} %get-tuple-element.9.below), custom_call_target="tpu_custom_call" | custom-call | tf_op jit(solution)/shard_map/pallas_call | solution.py:348
Async XLA Ops:
  0.6 1.4 %copy-start = (f32[96,32,128]{2,1,0:T(8,128)S(1)}, f32[96,32,128]{2,1,0:T(8,128)}, u32[]{:S(2)}) copy-start(f32[96,32,128]{2,1,0:T(8,128)} %param.2) | copy-start | bytes 4718596
  2.0 1.4 %copy-start.1 = (f32[96,32,128]{2,1,0:T(8,128)S(1)}, f32[96,32,128]{2,1,0:T(8,128)}, u32[]{:S(2)}) copy-start(f32[96,32,128]{2,1,0:T(8,128)} %param.3) | copy-start | bytes 4718596

commit v3 on v2

--- a/solution.py
+++ b/solution.py
@@ -129,7 +129,8 @@
                 def _():
                     row_send[s, side] = buf[p, pl.ds((1 + y) * width, width)]
                     row_copy(s, side).start()
-        for side, there in ((0, has_left), (1, has_right)):
+        odd = lax.rem(col, 2) == 1
+        for side, there in ((0, has_left & jnp.logical_not(odd)), (1, has_right), (0, has_left & odd)):
             @pl.when(there)
             def _():
                 col_copy(s, side, r).start()
@@ -242,7 +243,7 @@
             pair_sum[rows] = total[rows] + pair_recv[rows]
         else:
             pair_sum[rows] = total[rows]
-        for gap in range(1, groups):
+        for gap in range(groups - 1, 0, -1):
             @pl.when(group + gap < groups)
             def _():
                 group_copy(gap, r).start()

time: 38.2 us -> 38.2 us (level)
  no operation moved by 1% of the time
where the time goes in v3:
time: 38.2 us; the launch traced here: 38.1 us
  Pallas kernels  34.6 us (91%)
  local copies, waits for them, and re-layouts  2.81 us (7%)
  between operations  0.65 us (2%)
    pallas_call x1, Pallas kernels, body(): pl.pallas_call(functools.partial(kernel, (height, width, n_rows, n_cols))...  32.9 us
    unnamed x4, local copies, waits for them, and re-layouts  2.81 us
    pallas_call x1, Pallas kernels, body(): pl.pallas_call(functools.partial(finish, (height, width, n_cols)), out_sh...  1.71 us

profile of v3, /device:TPU:0, one launch (start us, length us, event | category | flops | bytes accessed | tf_op | source)
XLA Modules:
  0.0 38.1 jit_solution(16172247947873614239)
XLA Ops:
  0.6 0.0 copy-start
  0.6 1.4 %copy-done = f32[96,32,128]{2,1,0:T(8,128)S(1)} copy-done((f32[96,32,128]{2,1,0:T(8,128)S(1)}, f32[96,32,128]{2,1,0:T(8,128)}, u32[]{:S(2)}) %copy-start) | copy-done | bytes 1572888
  2.0 0.0 copy-start.1
  2.0 1.4 %copy-done.1 = f32[96,32,128]{2,1,0:T(8,128)S(1)} copy-done((f32[96,32,128]{2,1,0:T(8,128)S(1)}, f32[96,32,128]{2,1,0:T(8,128)}, u32[]{:S(2)}) %copy-start.1) | copy-done | bytes 1572888
  3.4 32.9 %shard_map.41 = (f32[3072,128]{1,0:T(8,128)S(1)}, f32[3072,128]{1,0:T(8,128)S(1)}, f32[96,128]{1,0:T(8,128)S(1)}) custom-call(f32[3072,128]{1,0:T(8,128)S(1)} %bitcast.4, f32[3072,128]{1,0:T(8,128)S(1)} %bitcast.5), custom_call_target="tpu_custom_call" | custom-call | tf_op jit(solution)/shard_map/pallas_call | solution.py:320
  36.4 1.7 %shard_map.42 = (f32[3072,128]{1,0:T(8,128)}, f32[3072,128]{1,0:T(8,128)}) custom-call(f32[3072,128]{1,0:T(8,128)S(1)} %get-tuple-element.7.end, f32[3072,128]{1,0:T(8,128)S(1)} %get-tuple-element.8.here, f32[96,128]{1,0:T(8,128)S(1)} %get-tuple-element.9.below), custom_call_target="tpu_custom_call" | custom-call | tf_op jit(solution)/shard_map/pallas_call | solution.py:349
Async XLA Ops:
  0.6 1.4 %copy-start = (f32[96,32,128]{2,1,0:T(8,128)S(1)}, f32[96,32,128]{2,1,0:T(8,128)}, u32[]{:S(2)}) copy-start(f32[96,32,128]{2,1,0:T(8,128)} %param.2) | copy-start | bytes 4718596
  2.0 1.4 %copy-start.1 = (f32[96,32,128]{2,1,0:T(8,128)S(1)}, f32[96,32,128]{2,1,0:T(8,128)}, u32[]{:S(2)}) copy-start(f32[96,32,128]{2,1,0:T(8,128)} %param.3) | copy-start | bytes 4718596
